TPU v7x, 256 devices: a whole 4x4x8 slice. The times are simulated.
256 devices in a mesh: pts: 32 (over x, z), grp: 8 (over y, core).
Axes of the slice: x: 4, y: 4, z: 8, core: 2. Of those that a mesh axis runs over, the one named last changes fastest.
Arguments:
- embeddings: bfloat16 [1048576, 1024], P(('pts', 'grp')), as said below
- best_start: float32 [1048576], P(('pts', 'grp')), may hold values from 0 to 2
- bounds_start: float32 [1048576], P(('pts', 'grp')), may hold values from 0 to 4
- proposals: int32 [8, 32], replicated, may hold values from 0 to 1048575
Outputs:
- gain_table: float32 [8, 32], replicated
- coverage: float32 [8], replicated
- best_final: float32 [1048576], P(('pts', 'grp'))
- bounds_final: float32 [1048576], P(('pts', 'grp'))
Inputs may be any that keep to these rules, and one draw needn't show every extreme that they name: Rows are real valued embeddings of varying norm.
All inputs are finite; a program needn't handle non-finite values.
Results may differ from a plain program's by a relative error of at most 0.0003.
Values may be sent and summed in bfloat16 or wider, within the bound.
No kernel may reach another device: no remote copies, remote signals or barrier semaphores. Data moves between devices by JAX's collectives and lax.ppermute only.
A program may use at most 64 MiB of HBM per device.

v0:
```python
import jax
import jax.numpy as jnp
from jax import lax
from jax.sharding import Mesh
from jax.sharding import PartitionSpec as P

STEPS = 8
PTS_GRP = ("pts_0", "pts_1", "grp_0", "grp_1")


def padded_to(lines, devices):
    spare = -len(lines) % devices
    return jnp.pad(lines, [(0, spare)] + [(0, 0)] * (lines.ndim - 1))


def copy_for_each(array, axis):
    copies = jnp.broadcast_to(array, (lax.axis_size(axis), *array.shape))
    return lax.all_to_all(copies, axis, split_axis=0, concat_axis=0, tiled=True)


def joined_along(tiles, dim):
    tiles = jnp.moveaxis(tiles, 0, dim)
    shape = tiles.shape
    return tiles.reshape(*shape[:dim], shape[dim] * shape[dim + 1], *shape[dim + 2 :])


def gather_axes(array, axes, dim):
    far, near = axes
    initial = copy_for_each(array, far)
    tiles = jnp.swapaxes(copy_for_each(initial, near), 0, 1)
    return joined_along(tiles.reshape(-1, *array.shape), dim)


def split_up(array, dim, devices):
    before, after = (array.shape[:dim], array.shape[dim + 1 :])
    return jnp.moveaxis(array.reshape(*before, devices, -1, *after), dim, 0)


def summed_on_arrival(array, axis, dim):
    devices = lax.axis_size(axis)
    tiles = lax.all_to_all(split_up(array, dim, devices), axis, 0, 0, tiled=True)
    return jnp.sum(tiles, axis=0)


def summed_rows(array, axes, dim):
    far, near = axes
    own = summed_on_arrival(split_up(array, dim, lax.axis_size(far)), near, dim + 1)
    return jnp.sum(lax.all_to_all(own, far, 0, 0, tiled=True), axis=0)


def nested_sum(array, axes):
    lines = array.reshape(-1, array.shape[-1])
    padded = padded_to(lines, lax.axis_size(axes[0]) * lax.axis_size(axes[1]))
    whole = gather_axes(summed_rows(padded, axes, 0), axes, 0)
    return lax.slice_in_dim(whole, 0, len(lines)).reshape(array.shape)


def taken_together(array, axis):
    everything = copy_for_each(array, axis)
    return jnp.sum(everything, axis=0)


def by_axis(array, axes):
    far, near = axes
    return taken_together(taken_together(array, near), far)


def together(arrays, axis):
    ends = [0]
    for a in arrays:
        ends.append(ends[-1] + a.size)
    subtotal = by_axis(jnp.concatenate([a.ravel() for a in arrays]), axis)
    return tuple((subtotal[b:e].reshape(a.shape) for a, b, e in zip(arrays, ends, ends[1:])))


def on_device(embeddings, best_start, bounds_start, proposals):
    row_count = embeddings.shape[0]
    prop_count = proposals.shape[1]
    own_index = lax.axis_index(PTS_GRP)
    first_row = own_index * row_count
    point_total = row_count * lax.axis_size(PTS_GRP)
    local_ids = first_row + jnp.arange(row_count, dtype=jnp.int32)
    best_sim = best_start
    bounds = bounds_start
    gain_rows = []
    cover_rows = []
    flat_chosen = proposals.reshape(-1)
    flat_offset = flat_chosen - first_row
    flat_owned = (flat_offset >= 0) & (flat_offset < row_count)
    all_rows = jnp.take(embeddings, jnp.clip(flat_offset, 0, row_count - 1), axis=0)
    all_masked = jnp.where(flat_owned[:, None], all_rows, jnp.zeros_like(all_rows)).astype(
        jnp.float32
    )
    fetched_all = nested_sum(all_masked, (("pts_0", "pts_1"), ("grp_0", "grp_1"))).astype(
        jnp.bfloat16
    )
    similarity_all = lax.dot_general(
        embeddings, fetched_all, (((1,), (1,)), ((), ())), preferred_element_type=jnp.float32
    )
    for step_index in range(STEPS):
        chosen = proposals[step_index]
        similarity = similarity_all[:, step_index * prop_count : (step_index + 1) * prop_count]
        clipped = jnp.maximum(similarity - best_sim[:, None], 0.0)
        partial_sums = jnp.sum(clipped, axis=0)
        gain_sums, cover_total = together(
            (partial_sums, jnp.sum(best_sim)), (("pts_0", "pts_1"), ("grp_0", "grp_1"))
        )
        gain_values = gain_sums / point_total
        if step_index > 0:
            cover_rows.append(cover_total / point_total)
        weights = (gain_values + 0.01) / (jnp.sum(gain_values) + 0.01 * prop_count)
        mixed = jnp.dot(similarity, weights, precision=lax.Precision.HIGHEST)
        best_sim = jnp.maximum(best_sim, mixed)
        matches = local_ids[:, None] == chosen[None, :]
        refreshed = jnp.max(jnp.where(matches, gain_values[None, :], -1.0), axis=1)
        bounds = jnp.where(jnp.any(matches, axis=1), refreshed, bounds)
        gain_rows.append(gain_values)
    cover_rows.append(
        by_axis(jnp.sum(best_sim), (("pts_0", "pts_1"), ("grp_0", "grp_1"))) / point_total
    )
    return (jnp.stack(gain_rows), jnp.stack(cover_rows), best_sim, bounds)


def solution(mesh):
    torus = Mesh(mesh.devices.reshape(4, 8, 4, 2), ("pts_0", "pts_1", "grp_0", "grp_1"))
    in_specs = (P(PTS_GRP, None), P(PTS_GRP), P(PTS_GRP), P())
    out_specs = (P(), P(), P(PTS_GRP), P(PTS_GRP))
    return jax.shard_map(
        on_device, mesh=torus, in_specs=in_specs, out_specs=out_specs, check_vma=False
    )
```

profile of v0, /device:TPU:8, one launch (start us, length us, event | category | flops | bytes accessed | tf_op | source)
XLA Modules:
  0.0 329.6 jit_solution(12101067295538476097)
XLA Ops:
  2.5 6.0 %gather_fusion = bf16[256,1024]{1,0:T(8,128)(2,1)S(1)} fusion(bf16[4096,1024]{1,0:T(8,128)(2,1)} %param.4, s32[1024]{0:T(1024)S(1)} %pad_clamp_fusion), kind=kCustom, calls=%fused_computation | custom fusion | bytes 1049600 | tf_op jit(solution)/shard_map/jit(_take)/gather | solution.py:90
  9.1 19.3 %all_to_all.131 = f32[8,32,1,1024]{3,1,2,0:T(8,128)S(1)} all-to-all(f32[8,32,1,1024]{3,1,2,0:T(8,128)S(1)} %convert_bitcast_fusion), channel_id=1, replica_groups=mesh['pts_0'=4,'pts_1'=8,'grp_0'=4,'grp_1'=2] {'grp_0','grp_1'}, dimensions={0} | all-to-all | bytes 2097152 | tf_op jit(solution)/shard_map/all_to_all | solution.py:41
  28.6 21.5 %all_to_all.132 = f32[32,1,1024]{2,1,0:T(1,128)S(1)} all-to-all(f32[32,1,1024]{2,1,0:T(1,128)S(1)} %reduce_sum.408), channel_id=1, replica_groups=mesh['pts_0'=4,'pts_1'=8,'grp_0'=4,'grp_1'=2] {'pts_0','pts_1'}, dimensions={0} | all-to-all | bytes 262144 | tf_op jit(solution)/shard_map/all_to_all | solution.py:48
  51.8 13.5 %all_to_all.133 = bf16[32,2,512]{2,1,0:T(2,128)(2,1)S(1)} all-to-all(bf16[32,2,512]{2,1,0:T(2,128)(2,1)S(1)} %reshape.266), channel_id=1, replica_groups=mesh['pts_0'=4,'pts_1'=8,'grp_0'=4,'grp_1'=2] {'pts_0','pts_1'}, dimensions={0} | all-to-all | bytes 131072 | tf_op jit(solution)/shard_map/all_to_all | solution.py:18
  66.3 4.8 %all-to-all-start.3 = ((bf16[8,32,1,1024]{3,1,2,0:T(8,128)(2,1)}), bf16[8,32,1,1024]{3,1,2,0:T(8,128)(2,1)S(1)}, u32[]{:S(2)}, u32[]{:S(2)}) async-start(bf16[8,32,1,1024]{3,1,2,0:T(8,128)(2,1)} %broadcast_in_dim.165), calls=%async_computation.3 | async-start | bytes 1048576 | tf_op jit(solution)/shard_map/all_to_all | solution.py:18
  71.6 8.3 %all-to-all-done.3 = bf16[8,32,1,1024]{3,1,2,0:T(8,128)(2,1)S(1)} async-done(((bf16[8,32,1,1024]{3,1,2,0:T(8,128)(2,1)}), bf16[8,32,1,1024]{3,1,2,0:T(8,128)(2,1)S(1)}, u32[]{:S(2)}, u32[]{:S(2)}) %all-to-all-start.3) | async-done | bytes 524320 | tf_op jit(solution)/shard_map/all_to_all | solution.py:18
  79.9 5.9 %convolution_bitcast_fusion = f32[4096,256]{0,1:T(8,128)S(1)} fusion(bf16[4096,1024]{1,0:T(8,128)(2,1)} %param.4, bf16[8,32,1,1024]{3,1,2,0:T(8,128)(2,1)S(1)} %all-to-all-done.3), kind=kOutput, calls=%fused_computation.1 | convolution fusion | flops 2147483648 | bytes 13107200 | tf_op jit(solution)/shard_map/dot_general | solution.py:97
  88.6 7.6 %all_to_all.134 = f32[8,1,33]{2,1,0:T(1,128)S(1)} all-to-all(f32[8,1,33]{2,1,0:T(1,128)S(1)} %broadcast_in_dim.166), channel_id=1, replica_groups=mesh['pts_0'=4,'pts_1'=8,'grp_0'=4,'grp_1'=2] {'grp_0','grp_1'}, dimensions={0} | all-to-all | bytes 2112 | tf_op jit(solution)/shard_map/all_to_all | solution.py:18
  96.3 13.0 %all_to_all.135 = f32[32,1,33]{2,1,0:T(1,128)S(1)} all-to-all(f32[32,1,33]{2,1,0:T(1,128)S(1)} %broadcast_in_dim.167), channel_id=1, replica_groups=mesh['pts_0'=4,'pts_1'=8,'grp_0'=4,'grp_1'=2] {'pts_0','pts_1'}, dimensions={0} | all-to-all | bytes 8448 | tf_op jit(solution)/shard_map/all_to_all | solution.py:18
  114.5 7.6 %all_to_all.136 = f32[8,1,33]{2,1,0:T(1,128)S(1)} all-to-all(f32[8,1,33]{2,1,0:T(1,128)S(1)} %broadcast_in_dim.168), channel_id=1, replica_groups=mesh['pts_0'=4,'pts_1'=8,'grp_0'=4,'grp_1'=2] {'grp_0','grp_1'}, dimensions={0} | all-to-all | bytes 2112 | tf_op jit(solution)/shard_map/all_to_all | solution.py:18
  122.2 12.8 %all_to_all.137 = f32[32,1,33]{2,1,0:T(1,128)S(1)} all-to-all(f32[32,1,33]{2,1,0:T(1,128)S(1)} %broadcast_in_dim.169), channel_id=1, replica_groups=mesh['pts_0'=4,'pts_1'=8,'grp_0'=4,'grp_1'=2] {'pts_0','pts_1'}, dimensions={0} | all-to-all | bytes 8448 | tf_op jit(solution)/shard_map/all_to_all | solution.py:18
  140.2 7.6 %all_to_all.138 = f32[8,1,33]{2,1,0:T(1,128)S(1)} all-to-all(f32[8,1,33]{2,1,0:T(1,128)S(1)} %broadcast_in_dim.170), channel_id=1, replica_groups=mesh['pts_0'=4,'pts_1'=8,'grp_0'=4,'grp_1'=2] {'grp_0','grp_1'}, dimensions={0} | all-to-all | bytes 2112 | tf_op jit(solution)/shard_map/all_to_all | solution.py:18
  147.9 12.8 %all_to_all.139 = f32[32,1,33]{2,1,0:T(1,128)S(1)} all-to-all(f32[32,1,33]{2,1,0:T(1,128)S(1)} %broadcast_in_dim.171), channel_id=1, replica_groups=mesh['pts_0'=4,'pts_1'=8,'grp_0'=4,'grp_1'=2] {'pts_0','pts_1'}, dimensions={0} | all-to-all | bytes 8448 | tf_op jit(solution)/shard_map/all_to_all | solution.py:18
  165.9 7.6 %all_to_all.140 = f32[8,1,33]{2,1,0:T(1,128)S(1)} all-to-all(f32[8,1,33]{2,1,0:T(1,128)S(1)} %broadcast_in_dim.172), channel_id=1, replica_groups=mesh['pts_0'=4,'pts_1'=8,'grp_0'=4,'grp_1'=2] {'grp_0','grp_1'}, dimensions={0} | all-to-all | bytes 2112 | tf_op jit(solution)/shard_map/all_to_all | solution.py:18
  173.6 12.8 %all_to_all.141 = f32[32,1,33]{2,1,0:T(1,128)S(1)} all-to-all(f32[32,1,33]{2,1,0:T(1,128)S(1)} %broadcast_in_dim.173), channel_id=1, replica_groups=mesh['pts_0'=4,'pts_1'=8,'grp_0'=4,'grp_1'=2] {'pts_0','pts_1'}, dimensions={0} | all-to-all | bytes 8448 | tf_op jit(solution)/shard_map/all_to_all | solution.py:18
  191.6 7.6 %all_to_all.142 = f32[8,1,33]{2,1,0:T(1,128)S(1)} all-to-all(f32[8,1,33]{2,1,0:T(1,128)S(1)} %broadcast_in_dim.174), channel_id=1, replica_groups=mesh['pts_0'=4,'pts_1'=8,'grp_0'=4,'grp_1'=2] {'grp_0','grp_1'}, dimensions={0} | all-to-all | bytes 2112 | tf_op jit(solution)/shard_map/all_to_all | solution.py:18
  199.3 12.8 %all_to_all.143 = f32[32,1,33]{2,1,0:T(1,128)S(1)} all-to-all(f32[32,1,33]{2,1,0:T(1,128)S(1)} %broadcast_in_dim.175), channel_id=1, replica_groups=mesh['pts_0'=4,'pts_1'=8,'grp_0'=4,'grp_1'=2] {'pts_0','pts_1'}, dimensions={0} | all-to-all | bytes 8448 | tf_op jit(solution)/shard_map/all_to_all | solution.py:18
  217.3 7.6 %all_to_all.144 = f32[8,1,33]{2,1,0:T(1,128)S(1)} all-to-all(f32[8,1,33]{2,1,0:T(1,128)S(1)} %broadcast_in_dim.176), channel_id=1, replica_groups=mesh['pts_0'=4,'pts_1'=8,'grp_0'=4,'grp_1'=2] {'grp_0','grp_1'}, dimensions={0} | all-to-all | bytes 2112 | tf_op jit(solution)/shard_map/all_to_all | solution.py:18
  225.0 12.8 %all_to_all.145 = f32[32,1,33]{2,1,0:T(1,128)S(1)} all-to-all(f32[32,1,33]{2,1,0:T(1,128)S(1)} %broadcast_in_dim.177), channel_id=1, replica_groups=mesh['pts_0'=4,'pts_1'=8,'grp_0'=4,'grp_1'=2] {'pts_0','pts_1'}, dimensions={0} | all-to-all | bytes 8448 | tf_op jit(solution)/shard_map/all_to_all | solution.py:18
  243.0 7.6 %all_to_all.146 = f32[8,1,33]{2,1,0:T(1,128)S(1)} all-to-all(f32[8,1,33]{2,1,0:T(1,128)S(1)} %broadcast_in_dim.178), channel_id=1, replica_groups=mesh['pts_0'=4,'pts_1'=8,'grp_0'=4,'grp_1'=2] {'grp_0','grp_1'}, dimensions={0} | all-to-all | bytes 2112 | tf_op jit(solution)/shard_map/all_to_all | solution.py:18
  255.2 9.7 %all-to-all-done.17 = f32[32,1,33]{2,1,0:T(1,128)S(1)} async-done(((f32[32,1,33]{2,1,0:T(1,128)}), f32[32,1,33]{2,1,0:T(1,128)S(1)}, u32[]{:S(2)}, u32[]{:S(2)}) %all-to-all-start.17) | async-done | bytes 4256 | tf_op jit(solution)/shard_map/all_to_all | solution.py:18
  270.7 4.7 %all-to-all-start.18 = ((f32[8,1,33]{2,1,0:T(1,128)}), f32[8,1,33]{2,1,0:T(1,128)S(1)}, u32[]{:S(2)}, u32[]{:S(2)}) async-start(f32[8,1,33]{2,1,0:T(1,128)} %broadcast_in_dim.180), calls=%async_computation.18 | async-start | bytes 8192 | tf_op jit(solution)/shard_map/all_to_all | solution.py:18
  309.5 8.4 %all-to-all-start.21 = ((f32[32,1,1]{2,1,0:T(1,128)}), f32[32,1,1]{2,1,0:T(1,128)S(1)}, u32[]{:S(2)}, u32[]{:S(2)}) async-start(f32[32,1,1]{2,1,0:T(1,128)} %broadcast_in_dim.183), calls=%async_computation.21 | async-start | bytes 32768 | tf_op jit(solution)/shard_map/all_to_all | solution.py:18
  318.5 9.2 %all-to-all-done.21 = f32[32,1,1]{2,1,0:T(1,128)S(1)} async-done(((f32[32,1,1]{2,1,0:T(1,128)}), f32[32,1,1]{2,1,0:T(1,128)S(1)}, u32[]{:S(2)}, u32[]{:S(2)}) %all-to-all-start.21) | async-done | bytes 160 | tf_op jit(solution)/shard_map/all_to_all | solution.py:18
  (126 shorter events, 76.7 us)
Async XLA Ops:
  8.5 62.6 %copy-start.1 = (f32[4096]{0:T(1024)S(1)}, f32[4096]{0:T(1024)}, u32[]{:S(2)}) copy-start(f32[4096]{0:T(1024)} %param.5) | copy-start | bytes 49156
  66.3 13.7 %all-to-all-start.3 = ((bf16[8,32,1,1024]{3,1,2,0:T(8,128)(2,1)}), bf16[8,32,1,1024]{3,1,2,0:T(8,128)(2,1)S(1)}, u32[]{:S(2)}, u32[]{:S(2)}) async-start(bf16[8,32,1,1024]{3,1,2,0:T(8,128)(2,1)} %broadcast_in_dim.165), calls=%async_computation.3 | async-start | bytes 1048576 | tf_op jit(solution)/shard_map/all_to_all | solution.py:18
  85.8 1.9 copy-start
  87.7 167.4 %copy-start.2 = (s32[8,32]{1,0:T(8,128)S(1)}, s32[8,32]{1,0:T(8,128)}, u32[]{:S(2)}) copy-start(s32[8,32]{1,0:T(8,128)} %param.7) | copy-start | bytes 3076
  135.0 170.2 %copy-start.3 = (f32[4096]{0:T(1024)S(1)}, f32[4096]{0:T(1024)}, u32[]{:S(2)}) copy-start(f32[4096]{0:T(1024)} %param.6) | copy-start | bytes 49156
  251.3 13.6 %all-to-all-start.17 = ((f32[32,1,33]{2,1,0:T(1,128)}), f32[32,1,33]{2,1,0:T(1,128)S(1)}, u32[]{:S(2)}, u32[]{:S(2)}) async-start(f32[32,1,33]{2,1,0:T(1,128)} %broadcast_in_dim.179), calls=%async_computation.17 | async-start | bytes 32768 | tf_op jit(solution)/shard_map/all_to_all | solution.py:18
  270.7 8.5 %all-to-all-start.18 = ((f32[8,1,33]{2,1,0:T(1,128)}), f32[8,1,33]{2,1,0:T(1,128)S(1)}, u32[]{:S(2)}, u32[]{:S(2)}) async-start(f32[8,1,33]{2,1,0:T(1,128)} %broadcast_in_dim.180), calls=%async_computation.18 | async-start | bytes 8192 | tf_op jit(solution)/shard_map/all_to_all | solution.py:18
  279.8 13.6 %all-to-all-start.19 = ((f32[32,1,33]{2,1,0:T(1,128)}), f32[32,1,33]{2,1,0:T(1,128)S(1)}, u32[]{:S(2)}, u32[]{:S(2)}) async-start(f32[32,1,33]{2,1,0:T(1,128)} %broadcast_in_dim.181), calls=%async_computation.19 | async-start | bytes 32768 | tf_op jit(solution)/shard_map/all_to_all | solution.py:18
  299.2 8.5 %all-to-all-start.20 = ((f32[8,1,1]{2,1,0:T(1,128)}), f32[8,1,1]{2,1,0:T(1,128)S(1)}, u32[]{:S(2)}, u32[]{:S(2)}) async-start(f32[8,1,1]{2,1,0:T(1,128)} %broadcast_in_dim.182), calls=%async_computation.20 | async-start | bytes 8192 | tf_op jit(solution)/shard_map/all_to_all | solution.py:18
  309.5 18.2 %all-to-all-start.21 = ((f32[32,1,1]{2,1,0:T(1,128)}), f32[32,1,1]{2,1,0:T(1,128)S(1)}, u32[]{:S(2)}, u32[]{:S(2)}) async-start(f32[32,1,1]{2,1,0:T(1,128)} %broadcast_in_dim.183), calls=%async_computation.21 | async-start | bytes 32768 | tf_op jit(solution)/shard_map/all_to_all | solution.py:18
where the time goes:
time: 332 us; the launch traced here: 330 us
  blocking collectives  185 us (56%)
  waiting for transfers between devices  34.1 us (10%)
  other arithmetic  32.3 us (10%)
  starting transfers between devices  30.2 us (9%)
  local copies, waits for them, and re-layouts  19.7 us (6%)
  matrix products  17.3 us (5%)
  between operations  11.3 us (3%)
    all_to_all x14, blocking collectives, copy_for_each(): return lax.all_to_all(copies, axis, split_axis=0, concat_axis=0, tiled=True)  144 us
    all_to_all x6, waiting for transfers between devices, copy_for_each(): return lax.all_to_all(copies, axis, split_axis=0, concat_axis=0, tiled=True)  34.1 us
    all_to_all x6, starting transfers between devices, copy_for_each(): return lax.all_to_all(copies, axis, split_axis=0, concat_axis=0, tiled=True)  30.2 us
    all_to_all x1, blocking collectives, summed_rows(): return jnp.sum(lax.all_to_all(own, far, 0, 0, tiled=True), axis=0)  21.5 us
    all_to_all x1, blocking collectives, summed_on_arrival(): lax.all_to_all(split_up(array, dim, devices), axis, 0, 0, tiled=True)  19.3 us
    dot_general x8, matrix products, on_device(): mixed = jnp.dot(similarity, weights, precision=lax.Precision.HIGHEST)  11.4 us
    reduce_sum x8, other arithmetic, on_device(): partial_sums = jnp.sum(clipped, axis=0)  8.57 us
  transfers between devices with their start and end apart: 6, of which 6 were waited for; matrix products, arithmetic and copies ran while one was open for 2% of the time, Pallas kernels for 0%

commit v1 on v0

v1 whole, which is shorter than its diff:
```python
import functools

import jax
import jax.numpy as jnp
from jax import lax
from jax.experimental import pallas as pl
from jax.experimental.pallas import tpu as pltpu
from jax.sharding import Mesh
from jax.sharding import PartitionSpec as P

AXES = ("x", "z", "y", "core")
VMEM = pl.BlockSpec(memory_space=pltpu.VMEM)
SMEM = pl.BlockSpec(memory_space=pltpu.SMEM)
ANY = pl.BlockSpec(memory_space=pl.ANY)
LANES = 128
SUB = 8
GRANT = 12 << 20
STREAM_GRANT = 48 << 20
CHUNK = 512


def shape_of(shape, dtype=jnp.float32):
    return jax.ShapeDtypeStruct(shape, dtype)


def rows_kernel(offsets, points, out, blocks, rows, arrived):
    count, row_total = out.shape[0], points.shape[0]

    def owned(k):
        return (offsets[k] >= 0) & (offsets[k] < row_total)

    def copy(k):
        base = pl.multiple_of(lax.shift_right_logical(offsets[k], 3) * SUB, SUB)
        return pltpu.make_async_copy(points.at[pl.ds(base, SUB)], blocks.at[k], arrived.at[k])

    def start(k, carry):
        @pl.when(owned(k))
        def _():
            copy(k).start()

        return carry

    def take(k, carry):
        @pl.when(owned(k))
        def _():
            copy(k).wait()
            block = blocks[k].astype(jnp.float32)
            line = lax.broadcasted_iota(jnp.int32, block.shape, 0)
            mine = jnp.where(line == (offsets[k] & (SUB - 1)), block, 0.0)
            rows[pl.ds(k, 1), :] = jnp.sum(mine, axis=0, keepdims=True)

        return carry

    lax.fori_loop(0, count, start, 0, unroll=8)
    rows[...] = jnp.zeros_like(rows)
    lax.fori_loop(0, count, take, 0, unroll=8)
    out[...] = rows[...].astype(out.dtype)


def own_rows(offsets, points):
    count, width = offsets.shape[0], points.shape[1]
    return pl.pallas_call(
        rows_kernel,
        out_shape=shape_of((count, width), points.dtype),
        in_specs=[SMEM, ANY],
        out_specs=VMEM,
        scratch_shapes=[
            pltpu.VMEM((count, SUB, width), points.dtype),
            pltpu.VMEM((count, width), jnp.float32),
            pltpu.SemaphoreType.DMA((count,)),
        ],
        compiler_params=pltpu.CompilerParams(vmem_limit_bytes=STREAM_GRANT),
    )(offsets, points)


def as_column(row, height):
    line = lax.broadcasted_iota(jnp.int32, (height, LANES), 0)
    lane = lax.broadcasted_iota(jnp.int32, (height, LANES), 1)
    spread = jnp.where(line == lane, jnp.broadcast_to(row, (height, LANES)), 0.0)
    return jnp.sum(spread, axis=1, keepdims=True)


def as_row(column):
    height = column.shape[0]
    line = lax.broadcasted_iota(jnp.int32, (height, LANES), 0)
    lane = lax.broadcasted_iota(jnp.int32, (height, LANES), 1)
    return jnp.sum(jnp.where(line == lane, column, 0.0), axis=0, keepdims=True)


def every_sublane(tile):
    for shift in (4, 2, 1):
        tile = tile + pltpu.roll(tile, shift, 0)
    return tile


def shares(gained, cover, props):
    lane = lax.broadcasted_iota(jnp.int32, (1, LANES), 1)
    row = as_row(jnp.sum(gained, axis=1, keepdims=True))
    total = jnp.sum(cover[:1], axis=1, keepdims=True)
    return jnp.where(lane == props, total, row)


def first_kernel(props, fetched, points, best, similarity, out, held, arrived):
    width = best.shape[1]
    chunks = []
    for i in range(0, width, CHUNK):
        part = pl.ds(i, CHUNK)
        chunks.append(pltpu.make_async_copy(points.at[part], held.at[part], arrived.at[i // CHUNK]))
        chunks[-1].start()
    gained = jnp.zeros((props, LANES), jnp.float32)
    for i, chunk in zip(range(0, width, CHUNK), chunks):
        chunk.wait()
        similarity[:, i : i + CHUNK] = lax.dot_general(
            fetched[...],
            held[i : i + CHUNK, :],
            (((1,), (1,)), ((), ())),
            preferred_element_type=jnp.float32,
        )
        for j in range(i, i + CHUNK, LANES):
            cols = slice(j, j + LANES)
            gained += jnp.maximum(similarity[0:props, cols] - best[:, cols], 0.0)
    row = shares(gained, jnp.zeros((SUB, LANES), jnp.float32), props)
    out[...] = jnp.broadcast_to(row, out.shape)


def first_call(props, fetched, points, best, devices):
    return pl.pallas_call(
        functools.partial(first_kernel, props),
        out_shape=[shape_of((fetched.shape[0], best.shape[1])), shape_of((devices, LANES))],
        in_specs=[VMEM, ANY, VMEM],
        out_specs=[VMEM, VMEM],
        scratch_shapes=[
            pltpu.VMEM(points.shape, points.dtype),
            pltpu.SemaphoreType.DMA((points.shape[0] // CHUNK,)),
        ],
        compiler_params=pltpu.CompilerParams(vmem_limit_bytes=STREAM_GRANT),
    )(fetched, points, best)


def step_kernel(step, props, point_total, parts, similarity, best, table, new_best, new_table, out=None):
    width = best.shape[1]
    last = out is None
    lane = lax.broadcasted_iota(jnp.int32, (1, LANES), 1)
    line = lax.broadcasted_iota(jnp.int32, table.shape, 0)
    gains = jnp.sum(parts[...], axis=0, keepdims=True) / point_total
    new_table[...] = jnp.where(line == step, gains, table[...])
    total = jnp.sum(jnp.where(lane < props, gains, 0.0), axis=1, keepdims=True)
    weight = as_column((gains + 0.01) / (total + 0.01 * props), props)
    weights = jnp.broadcast_to(weight, (props, LANES))
    here = slice(step * props, (step + 1) * props)
    following = slice((step + 1) * props, (step + 2) * props)
    gained = jnp.zeros((props, LANES), jnp.float32)
    cover = jnp.zeros((SUB, LANES), jnp.float32)
    for j in range(width // LANES):
        cols = slice(j * LANES, (j + 1) * LANES)
        product = similarity[here, cols] * weights
        mixed = product[0:SUB]
        for i in range(SUB, props, SUB):
            mixed = mixed + product[i : i + SUB]
        now = jnp.maximum(jnp.broadcast_to(best[:, cols], (SUB, LANES)), every_sublane(mixed))
        new_best[:, cols] = now[: new_best.shape[0]]
        cover += now
        if not last:
            ahead = jnp.concatenate([now] * (props // SUB), axis=0)
            gained += jnp.maximum(similarity[following, cols] - ahead, 0.0)
    return shares(gained, cover, props)


def middle_kernel(step, props, point_total, parts, similarity, best, table, new_best, new_table, out):
    row = step_kernel(step, props, point_total, parts, similarity, best, table, new_best, new_table, out)
    out[...] = jnp.broadcast_to(row, out.shape)


def last_kernel(step, props, point_total, parts, similarity, best, table, new_best, new_table, out):
    row = step_kernel(step, props, point_total, parts, similarity, best, table, new_best, new_table)
    out[...] = jnp.broadcast_to(row, out.shape)


def cover_kernel(props, point_total, parts, table, gain_table, coverage):
    steps = table.shape[0]
    gain_table[...] = table[:, 0:props]
    final = jnp.sum(parts[...], axis=0, keepdims=True) / point_total
    line = lax.broadcasted_iota(jnp.int32, table.shape, 0)
    lane = lax.broadcasted_iota(jnp.int32, table.shape, 1)
    ahead = jnp.where(line == steps - 1, final, pltpu.roll(table[...], steps - 1, 0))
    column = jnp.sum(jnp.where(lane == props, ahead, 0.0), axis=1, keepdims=True)
    coverage[...] = as_row(column)[:, 0:steps]


def bounds_kernel(offsets, table, bounds, out):
    steps, props = table.shape[0], offsets.shape[0] // table.shape[0]
    out[...] = bounds[...]
    row_total = out.shape[0] * LANES

    def put(k, carry):
        offset = offsets[k]

        @pl.when((offset >= 0) & (offset < row_total))
        def _():
            step, prop = lax.div(k, props), lax.rem(k, props)
            lane = lax.broadcasted_iota(jnp.int32, (1, LANES), 1)
            gains = table[pl.ds(step, 1), :]
            gain = jnp.sum(jnp.where(lane == prop, gains, 0.0), axis=1, keepdims=True)
            at = pl.ds(lax.shift_right_logical(offset, 7), 1)
            out[at, :] = jnp.where(lane == (offset & (LANES - 1)), gain, out[at, :])

        return carry

    lax.fori_loop(0, offsets.shape[0], put, 0, unroll=8)


def call(kernel, out_shape, in_specs):
    many = isinstance(out_shape, (tuple, list))
    return pl.pallas_call(
        kernel,
        out_shape=out_shape,
        in_specs=in_specs,
        out_specs=[VMEM] * len(out_shape) if many else VMEM,
        compiler_params=pltpu.CompilerParams(vmem_limit_bytes=GRANT),
    )


def every_part(parts):
    return lax.all_to_all(parts.reshape(parts.shape[0], 1, LANES), AXES, 0, 0, tiled=True).reshape(parts.shape)


def arrived_sum(rows, axes):
    tiles = lax.all_to_all(
        rows.reshape(lax.axis_size(axes), -1, rows.shape[1]), axes, 0, 0, tiled=True
    )
    return jnp.sum(tiles.astype(jnp.float32), axis=0).astype(rows.dtype)


def copies(rows, axes):
    sent = jnp.broadcast_to(rows, (lax.axis_size(axes), *rows.shape))
    return lax.all_to_all(sent, axes, 0, 0, tiled=True).reshape(-1, rows.shape[1])


def on_device(embeddings, best_start, bounds_start, proposals):
    row_count, devices = embeddings.shape[0], lax.axis_size(AXES)
    steps, props = proposals.shape
    point_total = row_count * devices
    offsets = proposals.reshape(-1) - lax.axis_index(AXES) * row_count

    rows = own_rows(offsets, embeddings)
    rows = arrived_sum(rows, ("x", "y", "core"))
    rows = arrived_sum(jnp.tile(rows, (lax.axis_size("z"), 1)), "z")
    fetched = copies(rows, ("x", "y", "core"))
    best = best_start.reshape(1, row_count)
    table = jnp.zeros((steps, LANES), jnp.float32)
    line = shape_of((devices, LANES))
    similarity, parts = first_call(props, fetched, embeddings, best, devices)
    for step in range(steps):
        parts = every_part(parts)
        last = step == steps - 1
        best, table, parts = call(
            functools.partial(last_kernel if last else middle_kernel, step, props, point_total),
            [shape_of((1 if last else SUB, row_count)), shape_of(table.shape), line],
            [VMEM] * 4,
        )(parts, similarity, best, table)
    bounds = call(bounds_kernel, shape_of((row_count // LANES, LANES)), [SMEM, VMEM, VMEM])(
        offsets, table, bounds_start.reshape(-1, LANES)
    )
    gain_table, coverage = call(
        functools.partial(cover_kernel, props, point_total),
        [shape_of((steps, props)), shape_of((1, steps))],
        [VMEM] * 2,
    )(every_part(parts), table)
    return gain_table, coverage.reshape(-1), best.reshape(-1), bounds.reshape(-1)


def solution(mesh):
    torus = Mesh(mesh.devices.reshape(4, 8, 4, 2), AXES)
    in_specs = (P(AXES, None), P(AXES), P(AXES), P())
    out_specs = (P(), P(), P(AXES), P(AXES))
    return jax.shard_map(
        on_device, mesh=torus, in_specs=in_specs, out_specs=out_specs, check_vma=False
    )
```

time: 332 us -> 235 us (0.71)
  other arithmetic: 32.3 us -> 0.8 us
  waiting for transfers between devices: 34.1 us -> 8.33 us
  starting transfers between devices: 30.2 us -> 6.4 us
  Pallas kernels: 0 us -> 20.4 us
  local copies, waits for them, and re-layouts: 19.7 us -> 0.15 us
  matrix products: 17.3 us -> 0 us
  blocking collectives: 185 us -> 196 us
  between operations: 11.3 us -> 0.76 us
    all_to_all x6 -> x1, waiting for transfers between devices: 34.1 us -> 8.33 us  [every_part(): lax.all_to_all(parts.reshape(parts.shape[0], 1, LANES), AXES, 0, 0, tiled...]
    all_to_all x6 -> x1, starting transfers between devices: 30.2 us -> 6.4 us  [every_part(): lax.all_to_all(parts.reshape(parts.shape[0], 1, LANES), AXES, 0, 0, tiled...]
    pallas_call x0 -> x12, Pallas kernels: none -> 20.4 us  [the longest x1 6.97 us: own_rows(): pl.pallas_call(rows_kernel, out_shape=shape_of((count, width), points.dty...]
    dot_general x9 -> x0, matrix products: 17.3 us -> none  [the longest x8 11.4 us: on_device(): mixed = jnp.dot(similarity, weights, precision=lax.Precision.HIGHEST)]
    reduce_sum x37 -> x2, other arithmetic: 16.3 us -> 0.11 us  [arrived_sum(): return jnp.sum(tiles.astype(jnp.float32), axis=0).astype(rows.dtype)]
    all_to_all x16 -> x11, blocking collectives: 185 us -> 196 us  [the longest x8 145 us: every_part(): lax.all_to_all(parts.reshape(parts.shape[0], 1, LANES), AXES, 0, 0, tiled...]
    gather x1 -> x0, local copies, waits for them, and re-layouts: 6.03 us -> none  [on_device(): jnp.take(embeddings, jnp.clip(flat_offset, 0, row_count - 1), axis=0)]
    broadcast_in_dim x21 -> x2, local copies, waits for them, and re-layouts: 5.88 us -> 0.05 us  [the longest x1 0.05 us: copies(): sent = jnp.broadcast_to(rows, (lax.axis_size(axes), *rows.shape))]
  transfers between devices with their start and end apart: 6 -> 1, of which waited for: 6 -> 1; matrix products, arithmetic and copies ran while one was open for 2% -> 0% of each run, Pallas kernels for 0% -> 2%
where the time goes in v1:
time: 235 us; the launch traced here: 232 us
  blocking collectives  196 us (83%)
  Pallas kernels  20.4 us (9%)
  waiting for transfers between devices  8.33 us (4%)
  starting transfers between devices  6.4 us (3%)
    all_to_all x8, blocking collectives, every_part(): lax.all_to_all(parts.reshape(parts.shape[0], 1, LANES), AXES, 0, 0, tiled...  145 us
    all_to_all x2, blocking collectives, arrived_sum(): lax.all_to_all(rows.reshape(lax.axis_size(axes), -1, rows.shape[1]), axes...  35.3 us
    all_to_all x1, blocking collectives, copies(): lax.all_to_all(sent, axes, 0, 0, tiled=True).reshape(-1, rows.shape[1])  14.8 us
    all_to_all x1, waiting for transfers between devices, every_part(): lax.all_to_all(parts.reshape(parts.shape[0], 1, LANES), AXES, 0, 0, tiled...  8.33 us
    pallas_call x1, Pallas kernels, own_rows(): pl.pallas_call(rows_kernel, out_shape=shape_of((count, width), points.dty...  6.97 us
    all_to_all x1, starting transfers between devices, every_part(): lax.all_to_all(parts.reshape(parts.shape[0], 1, LANES), AXES, 0, 0, tiled...  6.4 us
    pallas_call x1, Pallas kernels, first_call(): pl.pallas_call(functools.partial(first_kernel, props), out_shape=[shape_o...  5.1 us
  transfers between devices with their start and end apart: 1, of which 1 were waited for; matrix products, arithmetic and copies ran while one was open for 0% of the time, Pallas kernels for 2%

profile of v1, /device:TPU:8, one launch (start us, length us, event | category | flops | bytes accessed | tf_op | source)
XLA Modules:
  0.0 232.4 jit_solution(1827538300890168807)
XLA Ops:
  0.7 0.7 broadcast_subtract_fusion
  1.4 7.0 %shard_map.75 = bf16[256,1024]{1,0:T(8,128)(2,1)S(1)} custom-call(s32[256]{0:T(256)S(1)} %sub.10.offsets, bf16[4096,1024]{1,0:T(8,128)(2,1)} %points.3), custom_call_target="tpu_custom_call" | custom-call | tf_op jit(solution)/shard_map/pallas_call | solution.py:62
  8.4 17.4 %all_to_all.60 = bf16[32,8,1024]{2,1,0:T(8,128)(2,1)S(1)} all-to-all(bf16[32,8,1024]{2,1,0:T(8,128)(2,1)S(1)} %bitcast.44), channel_id=1, replica_groups=mesh['x'=4,'z'=8,'y'=4,'core'=2] {'x','y','core'}, dimensions={0} | all-to-all | bytes 1048576 | tf_op jit(solution)/shard_map/all_to_all | solution.py:228
  25.9 18.0 %all_to_all.61 = bf16[8,8,1024]{2,1,0:T(8,128)(2,1)S(1)} all-to-all(bf16[8,8,1024]{2,1,0:T(8,128)(2,1)S(1)} %reshape_tile.3), channel_id=1, replica_groups=mesh['x'=4,'z'=8,'y'=4,'core'=2] {'z'}, dimensions={0} | all-to-all | bytes 262144 | tf_op jit(solution)/shard_map/all_to_all | solution.py:228
  43.9 14.8 %all_to_all.62 = bf16[32,8,1024]{2,1,0:T(8,128)(2,1)S(1)} all-to-all(bf16[32,8,1024]{2,1,0:T(8,128)(2,1)S(1)} %broadcast_in_dim.6), channel_id=1, replica_groups=mesh['x'=4,'z'=8,'y'=4,'core'=2] {'x','y','core'}, dimensions={0} | all-to-all | bytes 1048576 | tf_op jit(solution)/shard_map/all_to_all | solution.py:236
  58.7 5.1 %shard_map.76 = (f32[256,4096]{1,0:T(8,128)S(1)}, f32[256,128]{1,0:T(8,128)S(1)}) custom-call(bf16[256,1024]{1,0:T(8,128)(2,1)S(1)} %bitcast.43, bf16[4096,1024]{1,0:T(8,128)(2,1)} %points.3, f32[1,4096]{1,0:T(1,128)S(1)} %bitcast.62), custom_call_target="tpu_custom_call" | custom-call | tf_op jit(solution)/shard_map/pallas_call | solution.py:127
  63.8 18.1 %all_to_all.63 = f32[256,1,128]{2,1,0:T(1,128)S(1)} all-to-all(f32[256,1,128]{2,1,0:T(1,128)S(1)} %bitcast.61), channel_id=1, replica_groups=mesh['x'=4,'z'=8,'y'=4,'core'=2] {'x','z','y','core'}, dimensions={0} | all-to-all | bytes 262144 | tf_op jit(solution)/shard_map/all_to_all | solution.py:224
  82.0 0.4 shard_map.77
  82.4 18.2 %all_to_all.64 = f32[256,1,128]{2,1,0:T(1,128)S(1)} all-to-all(f32[256,1,128]{2,1,0:T(1,128)S(1)} %bitcast.60), channel_id=1, replica_groups=mesh['x'=4,'z'=8,'y'=4,'core'=2] {'x','z','y','core'}, dimensions={0} | all-to-all | bytes 262144 | tf_op jit(solution)/shard_map/all_to_all | solution.py:224
  100.5 0.4 shard_map.78
  101.0 18.2 %all_to_all.65 = f32[256,1,128]{2,1,0:T(1,128)S(1)} all-to-all(f32[256,1,128]{2,1,0:T(1,128)S(1)} %bitcast.54), channel_id=1, replica_groups=mesh['x'=4,'z'=8,'y'=4,'core'=2] {'x','z','y','core'}, dimensions={0} | all-to-all | bytes 262144 | tf_op jit(solution)/shard_map/all_to_all | solution.py:224
  119.6 18.2 %all_to_all.66 = f32[256,1,128]{2,1,0:T(1,128)S(1)} all-to-all(f32[256,1,128]{2,1,0:T(1,128)S(1)} %bitcast.55), channel_id=1, replica_groups=mesh['x'=4,'z'=8,'y'=4,'core'=2] {'x','z','y','core'}, dimensions={0} | all-to-all | bytes 262144 | tf_op jit(solution)/shard_map/all_to_all | solution.py:224
  138.1 18.3 %all_to_all.67 = f32[256,1,128]{2,1,0:T(1,128)S(1)} all-to-all(f32[256,1,128]{2,1,0:T(1,128)S(1)} %bitcast.56), channel_id=1, replica_groups=mesh['x'=4,'z'=8,'y'=4,'core'=2] {'x','z','y','core'}, dimensions={0} | all-to-all | bytes 262144 | tf_op jit(solution)/shard_map/all_to_all | solution.py:224
  156.5 0.4 shard_map.81
  156.9 18.2 %all_to_all.68 = f32[256,1,128]{2,1,0:T(1,128)S(1)} all-to-all(f32[256,1,128]{2,1,0:T(1,128)S(1)} %bitcast.57), channel_id=1, replica_groups=mesh['x'=4,'z'=8,'y'=4,'core'=2] {'x','z','y','core'}, dimensions={0} | all-to-all | bytes 262144 | tf_op jit(solution)/shard_map/all_to_all | solution.py:224
  175.1 0.4 shard_map.82
  175.5 18.2 %all_to_all.69 = f32[256,1,128]{2,1,0:T(1,128)S(1)} all-to-all(f32[256,1,128]{2,1,0:T(1,128)S(1)} %bitcast.58), channel_id=1, replica_groups=mesh['x'=4,'z'=8,'y'=4,'core'=2] {'x','z','y','core'}, dimensions={0} | all-to-all | bytes 262144 | tf_op jit(solution)/shard_map/all_to_all | solution.py:224
  193.7 0.4 shard_map.83
  194.1 18.2 %all_to_all.70 = f32[256,1,128]{2,1,0:T(1,128)S(1)} all-to-all(f32[256,1,128]{2,1,0:T(1,128)S(1)} %bitcast.59), channel_id=1, replica_groups=mesh['x'=4,'z'=8,'y'=4,'core'=2] {'x','z','y','core'}, dimensions={0} | all-to-all | bytes 262144 | tf_op jit(solution)/shard_map/all_to_all | solution.py:224
  212.3 1.0 shard_map.84
  213.3 6.4 %all-to-all-start.11 = ((f32[256,1,128]{2,1,0:T(1,128)}), f32[256,1,128]{2,1,0:T(1,128)S(1)}, u32[]{:S(2)}, u32[]{:S(2)}) async-start(f32[256,1,128]{2,1,0:T(1,128)} %bitcast.28), calls=%async_computation.11 | async-start | bytes 262144 | tf_op jit(solution)/shard_map/all_to_all | solution.py:224
  219.7 3.7 %shard_map.86 = f32[32,128]{1,0:T(8,128)} custom-call(s32[256]{0:T(256)S(1)} %sub.10.offsets, f32[8,128]{1,0:T(8,128)S(1)} %get-tuple-element.56.table, f32[32,128]{1,0:T(8,128)S(1)} %bitcast.64), custom_call_target="tpu_custom_call" | custom-call | tf_op jit(solution)/shard_map/pallas_call | solution.py:261
  223.5 8.3 %all-to-all-done.11 = f32[256,1,128]{2,1,0:T(1,128)S(1)} async-done(((f32[256,1,128]{2,1,0:T(1,128)}), f32[256,1,128]{2,1,0:T(1,128)S(1)}, u32[]{:S(2)}, u32[]{:S(2)}) %all-to-all-start.11) | async-done | bytes 131104 | tf_op jit(solution)/shard_map/all_to_all | solution.py:224
  231.8 0.6 shard_map.85
  (12 shorter events, 1.1 us)
Async XLA Ops:
  0.6 58.1 %copy-start = (f32[4096]{0:T(1024)S(1)}, f32[4096]{0:T(1024)}, u32[]{:S(2)}) copy-start(f32[4096]{0:T(1024)} %param.5) | copy-start | bytes 49156
  156.5 63.2 %copy-start.1 = (f32[4096]{0:T(1024)S(1)}, f32[4096]{0:T(1024)}, u32[]{:S(2)}) copy-start(f32[4096]{0:T(1024)} %param.6) | copy-start | bytes 49156
  213.3 18.5 %all-to-all-start.11 = ((f32[256,1,128]{2,1,0:T(1,128)}), f32[256,1,128]{2,1,0:T(1,128)S(1)}, u32[]{:S(2)}, u32[]{:S(2)}) async-start(f32[256,1,128]{2,1,0:T(1,128)} %bitcast.28), calls=%async_computation.11 | async-start | bytes 262144 | tf_op jit(solution)/shard_map/all_to_all | solution.py:224

commit v2 on v1

v2 whole, which is shorter than its diff:
```python
import functools

import jax
import jax.numpy as jnp
from jax import lax
from jax.experimental import pallas as pl
from jax.experimental.pallas import tpu as pltpu
from jax.sharding import Mesh
from jax.sharding import PartitionSpec as P

AXIS = "device"
X, Z, Y, CORES = 4, 8, 4, 2
VMEM = pl.BlockSpec(memory_space=pltpu.VMEM)
SMEM = pl.BlockSpec(memory_space=pltpu.SMEM)
ANY = pl.BlockSpec(memory_space=pl.ANY)
LANES = 128
SUB = 8
GRANT = 12 << 20
ROWS_GRANT = 46 << 20
CHUNK = 512
WAITS = pl.CostEstimate(flops=200_000_000_000, bytes_accessed=1_000_000_000, transcendentals=0)


def shape_of(shape, dtype=jnp.float32):
    return jax.ShapeDtypeStruct(shape, dtype)


def first_row(row_total):
    return lax.axis_index(AXIS) * row_total


def rows_kernel(proposals, points, mine, others, owned, blocks, rows, arrived):
    row_total = points.shape[0]
    steps, props = proposals.shape
    half = mine.shape[0]
    lists, room = owned.shape
    first = first_row(row_total)

    def offset_of(k):
        return proposals[lax.div(k, props), lax.rem(k, props)] - first

    def note(i, found):
        found = list(found)
        for prop in range(props):
            for part in range(lists):
                step = part * (steps // lists) + i
                offset = proposals[step, prop] - first
                owned[part, found[part]] = step * props + prop
                found[part] += jnp.where((offset >= 0) & (offset < row_total), 1, 0)
        return tuple(found)

    def copy(k):
        base = pl.multiple_of(lax.shift_right_logical(offset_of(k), 3) * SUB, SUB)
        return pltpu.make_async_copy(points.at[pl.ds(base, SUB)], blocks.at[k], arrived.at[k])

    found = lax.fori_loop(0, steps // lists, note, (jnp.int32(0),) * lists)
    for part in range(lists):

        def start(i, carry, part=part):
            copy(owned[part, i]).start()
            return carry

        lax.fori_loop(0, found[part], start, 0)
    rows[...] = jnp.zeros_like(rows)
    for part in range(lists):

        def take(i, carry, part=part):
            k = owned[part, i]
            copy(k).wait()
            block = blocks[k].astype(jnp.float32)
            line = lax.broadcasted_iota(jnp.int32, block.shape, 0)
            row = jnp.where(line == (offset_of(k) & (SUB - 1)), block, 0.0)
            rows[pl.ds(k, 1), :] = jnp.sum(row, axis=0, keepdims=True)
            return carry

        lax.fori_loop(0, found[part], take, 0)
    core = lax.rem(lax.axis_index(AXIS), CORES)
    at = pl.multiple_of(core * half, half)
    mine[...] = rows[pl.ds(at, half), :].astype(mine.dtype)
    at = pl.multiple_of((1 - core) * half, half)
    others[...] = rows[pl.ds(at, half), :].astype(others.dtype)


def own_rows(proposals, points):
    count, width = proposals.size, points.shape[1]
    half = shape_of((count // CORES, width), points.dtype)
    return pl.pallas_call(
        rows_kernel,
        out_shape=[half, half],
        in_specs=[SMEM, ANY],
        out_specs=[VMEM, VMEM],
        scratch_shapes=[
            pltpu.SMEM((4, count // 4 + 1), jnp.int32),
            pltpu.VMEM((count, SUB, width), points.dtype),
            pltpu.VMEM((count, width), jnp.float32),
            pltpu.SemaphoreType.DMA((count,)),
        ],
        compiler_params=pltpu.CompilerParams(vmem_limit_bytes=ROWS_GRANT),
    )(proposals, points)


def pair_kernel(mine, arrived, out):
    out[...] = mine[...] + arrived[...]


def sum_kernel(tiles, out):
    total = tiles[0].astype(jnp.float32)
    for i in range(1, tiles.shape[0]):
        total += tiles[i].astype(jnp.float32)
    total = total.astype(out.dtype)
    for i in range(out.shape[0]):
        out[i] = total


def summed(tiles, copies):
    return call(sum_kernel, shape_of((copies, *tiles.shape[1:]), tiles.dtype), [VMEM], WAITS)(tiles)


def device(x, z, y, core):
    return ((x * Z + z) * Y + y) * CORES + core


PLANES = [[device(x, z, y, c) for x in range(X) for y in range(Y)] for z in range(Z) for c in range(CORES)]
LINES = [[device(x, z, y, c) for z in range(Z)] for x in range(X) for y in range(Y) for c in range(CORES)]
CHIPS = [(i, i ^ 1) for i in range(X * Z * Y * CORES)]


def back_and_forth(sizes):
    if not sizes:
        return [()]
    inner = back_and_forth(sizes[1:])
    return [(i, *rest) for i in range(sizes[0]) for rest in (inner if i % 2 == 0 else inner[::-1])]


ALL = [[device(x, z, y, c) for z, x, y, c in back_and_forth((Z, X, Y, CORES))]]


def exchanged(tiles, groups):
    return lax.all_to_all(tiles, AXIS, 0, 0, tiled=True, axis_index_groups=groups)


def from_other_core(rows):
    return lax.ppermute(rows, AXIS, CHIPS)


def as_column(row, height):
    line = lax.broadcasted_iota(jnp.int32, (height, LANES), 0)
    lane = lax.broadcasted_iota(jnp.int32, (height, LANES), 1)
    spread = jnp.where(line == lane, jnp.broadcast_to(row, (height, LANES)), 0.0)
    return jnp.sum(spread, axis=1, keepdims=True)


def as_row(column):
    height = column.shape[0]
    line = lax.broadcasted_iota(jnp.int32, (height, LANES), 0)
    lane = lax.broadcasted_iota(jnp.int32, (height, LANES), 1)
    return jnp.sum(jnp.where(line == lane, column, 0.0), axis=0, keepdims=True)


def every_sublane(tile):
    for shift in (4, 2, 1):
        tile = tile + pltpu.roll(tile, shift, 0)
    return tile


def shares(gained, cover, props):
    lane = lax.broadcasted_iota(jnp.int32, (1, LANES), 1)
    row = as_row(jnp.sum(gained, axis=1, keepdims=True))
    total = jnp.sum(cover[:1], axis=1, keepdims=True)
    return jnp.where(lane == props, total, row)


def first_kernel(props, mine, others, points, best, similarity, out, fetched):
    width, half = best.shape[1], mine.shape[0]
    core = lax.rem(lax.axis_index(AXIS), CORES)
    fetched[pl.ds(pl.multiple_of(core * half, half), half), :] = mine[...]
    fetched[pl.ds(pl.multiple_of((1 - core) * half, half), half), :] = others[...]
    gained = jnp.zeros((props, LANES), jnp.float32)
    for i in range(0, width, CHUNK):
        similarity[:, i : i + CHUNK] = lax.dot_general(
            fetched[...],
            points[i : i + CHUNK, :],
            (((1,), (1,)), ((), ())),
            preferred_element_type=jnp.float32,
        )
        for j in range(i, i + CHUNK, LANES):
            cols = slice(j, j + LANES)
            gained += jnp.maximum(similarity[0:props, cols] - best[:, cols], 0.0)
    row = shares(gained, jnp.zeros((SUB, LANES), jnp.float32), props)
    out[...] = jnp.broadcast_to(row, out.shape)


def step_kernel(step, props, point_total, parts, similarity, best, table, new_best, new_table, out=None):
    width = best.shape[1]
    last = out is None
    lane = lax.broadcasted_iota(jnp.int32, (1, LANES), 1)
    line = lax.broadcasted_iota(jnp.int32, table.shape, 0)
    gains = jnp.sum(parts[...], axis=0, keepdims=True) / point_total
    new_table[...] = jnp.where(line == step, gains, table[...])
    total = jnp.sum(jnp.where(lane < props, gains, 0.0), axis=1, keepdims=True)
    weight = as_column((gains + 0.01) / (total + 0.01 * props), props)
    weights = jnp.broadcast_to(weight, (props, LANES))
    here = slice(step * props, (step + 1) * props)
    following = slice((step + 1) * props, (step + 2) * props)
    gained = jnp.zeros((props, LANES), jnp.float32)
    cover = jnp.zeros((SUB, LANES), jnp.float32)
    for j in range(width // LANES):
        cols = slice(j * LANES, (j + 1) * LANES)
        product = similarity[here, cols] * weights
        mixed = product[0:SUB]
        for i in range(SUB, props, SUB):
            mixed = mixed + product[i : i + SUB]
        now = jnp.maximum(jnp.broadcast_to(best[:, cols], (SUB, LANES)), every_sublane(mixed))
        new_best[:, cols] = now[: new_best.shape[0]]
        cover += now
        if not last:
            ahead = jnp.concatenate([now] * (props // SUB), axis=0)
            gained += jnp.maximum(similarity[following, cols] - ahead, 0.0)
    return shares(gained, cover, props)


def middle_kernel(step, props, point_total, parts, similarity, best, table, new_best, new_table, out):
    row = step_kernel(step, props, point_total, parts, similarity, best, table, new_best, new_table, out)
    out[...] = jnp.broadcast_to(row, out.shape)


def last_kernel(step, props, point_total, parts, similarity, best, table, new_best, new_table, out):
    row = step_kernel(step, props, point_total, parts, similarity, best, table, new_best, new_table)
    out[...] = jnp.broadcast_to(row, out.shape)


def cover_kernel(props, point_total, parts, table, gain_table, coverage):
    steps = table.shape[0]
    gain_table[...] = table[:, 0:props]
    final = jnp.sum(parts[...], axis=0, keepdims=True) / point_total
    line = lax.broadcasted_iota(jnp.int32, table.shape, 0)
    lane = lax.broadcasted_iota(jnp.int32, table.shape, 1)
    ahead = jnp.where(line == steps - 1, final, pltpu.roll(table[...], steps - 1, 0))
    column = jnp.sum(jnp.where(lane == props, ahead, 0.0), axis=1, keepdims=True)
    coverage[...] = as_row(column)[:, 0:steps]


def bounds_kernel(proposals, table, bounds, out):
    steps, props = proposals.shape
    out[...] = bounds[...]
    row_total = out.shape[0] * LANES
    first = first_row(row_total)
    lane = lax.broadcasted_iota(jnp.int32, (1, LANES), 1)

    def put(step, carry):
        for prop in range(props):
            offset = proposals[step, prop] - first

            @pl.when((offset >= 0) & (offset < row_total))
            def _():
                gains = table[pl.ds(step, 1), :]
                gain = jnp.sum(jnp.where(lane == prop, gains, 0.0), axis=1, keepdims=True)
                at = pl.ds(lax.shift_right_logical(offset, 7), 1)
                out[at, :] = jnp.where(lane == (offset & (LANES - 1)), gain, out[at, :])

        return carry

    lax.fori_loop(0, steps, put, 0)


def call(kernel, out_shape, in_specs, cost=None, scratch=()):
    many = isinstance(out_shape, (tuple, list))
    return pl.pallas_call(
        kernel,
        out_shape=out_shape,
        in_specs=in_specs,
        out_specs=[VMEM] * len(out_shape) if many else VMEM,
        compiler_params=pltpu.CompilerParams(vmem_limit_bytes=GRANT),
        cost_estimate=cost,
        scratch_shapes=scratch,
    )


def every_part(parts):
    return exchanged(parts.reshape(parts.shape[0], 1, LANES), ALL).reshape(parts.shape)


def on_device(embeddings, best_start, bounds_start, proposals):
    row_count, devices = embeddings.shape[0], lax.axis_size(AXIS)
    steps, props = proposals.shape
    point_total = row_count * devices

    mine, others = own_rows(proposals, embeddings)
    half = shape_of(mine.shape, mine.dtype)
    tiles = call(pair_kernel, half, [VMEM] * 2)(mine, from_other_core(others))
    tiles = exchanged(tiles.reshape(X * Y, -1, mine.shape[1]), PLANES)
    tiles = exchanged(summed(tiles, Z), LINES)
    mine = exchanged(summed(tiles, X * Y), PLANES).reshape(mine.shape)
    others = from_other_core(mine)

    best = best_start.reshape(1, row_count)
    table = jnp.zeros((steps, LANES), jnp.float32)
    line = shape_of((devices, LANES))
    similarity, parts = call(
        functools.partial(first_kernel, props),
        [shape_of((steps * props, row_count)), line],
        [VMEM] * 4,
        scratch=[pltpu.VMEM((steps * props, mine.shape[1]), mine.dtype)],
    )(mine, others, embeddings, best)
    for step in range(steps):
        parts = every_part(parts)
        last = step == steps - 1
        best, table, parts = call(
            functools.partial(last_kernel if last else middle_kernel, step, props, point_total),
            [shape_of((1 if last else SUB, row_count)), shape_of(table.shape), line],
            [VMEM] * 4,
        )(parts, similarity, best, table)
    bounds = call(bounds_kernel, shape_of((row_count // LANES, LANES)), [SMEM, VMEM, VMEM])(
        proposals, table, bounds_start.reshape(-1, LANES)
    )
    gain_table, coverage = call(
        functools.partial(cover_kernel, props, point_total),
        [shape_of((steps, props)), shape_of((1, steps))],
        [VMEM] * 2,
    )(every_part(parts), table)
    return gain_table, coverage.reshape(-1), best.reshape(-1), bounds.reshape(-1)


def solution(mesh):
    line = Mesh(mesh.devices.reshape(-1), (AXIS,))
    in_specs = (P(AXIS, None), P(AXIS), P(AXIS), P())
    out_specs = (P(), P(), P(AXIS), P(AXIS))
    return jax.shard_map(
        on_device, mesh=line, in_specs=in_specs, out_specs=out_specs, check_vma=False
    )
```

time: 235 us -> 225 us (0.957)
  blocking collectives: 196 us -> 188 us
  Pallas kernels: 20.4 us -> 15 us
    all_to_all x11, blocking collectives: 196 us -> 188 us  [exchanged(): lax.all_to_all(tiles, AXIS, 0, 0, tiled=True, axis_index_groups=groups)]
    pallas_call x2 -> x5, Pallas kernels: 12.1 us -> 6.63 us  [the longest x1 4.12 us: own_rows(): pl.pallas_call(rows_kernel, out_shape=[half, half], in_specs=[SMEM, ANY],...]
    ppermute x0 -> x2, waiting for transfers between devices: none -> 2.69 us  [from_other_core(): return lax.ppermute(rows, AXIS, CHIPS)]
  transfers between devices with their start and end apart: 1 -> 3, of which waited for: 1 -> 3; matrix products, arithmetic and copies ran while one was open for 0% -> 0% of each run, Pallas kernels for 2% -> 2%
where the time goes in v2:
time: 225 us; the launch traced here: 222 us
  blocking collectives  188 us (84%)
  Pallas kernels  15 us (7%)
  waiting for transfers between devices  10.5 us (5%)
  starting transfers between devices  7.14 us (3%)
    all_to_all x11, blocking collectives, exchanged(): lax.all_to_all(tiles, AXIS, 0, 0, tiled=True, axis_index_groups=groups)  188 us
    all_to_all x1, waiting for transfers between devices, exchanged(): lax.all_to_all(tiles, AXIS, 0, 0, tiled=True, axis_index_groups=groups)  7.77 us
    all_to_all x1, starting transfers between devices, exchanged(): lax.all_to_all(tiles, AXIS, 0, 0, tiled=True, axis_index_groups=groups)  6.55 us
  transfers between devices with their start and end apart: 3, of which 3 were waited for; matrix products, arithmetic and copies ran while one was open for 0% of the time, Pallas kernels for 2%

profile of v2, /device:TPU:8, one launch (start us, length us, event | category | flops | bytes accessed | tf_op | source)
XLA Modules:
  0.0 221.6 jit_solution(16559915664682936072)
XLA Ops:
  0.6 0.7 copy-done.2
  1.3 4.1 %shard_map.75 = (bf16[128,1024]{1,0:T(8,128)(2,1)S(1)}, bf16[128,1024]{1,0:T(8,128)(2,1)S(1)}) custom-call(s32[8,32]{1,0:T(8,128)S(1)} %copy-done.2, bf16[4096,1024]{1,0:T(8,128)(2,1)} %points.3), custom_call_target="tpu_custom_call" | custom-call | tf_op jit(solution)/shard_map/pallas_call | solution.py:87
  5.5 0.6 collective-permute-start
  6.0 1.2 collective-permute-done.arrived
  7.2 15.1 %all_to_all.60.tiles = bf16[16,8,1024]{2,1,0:T(8,128)(2,1)S(1)} all-to-all(bf16[16,8,1024]{2,1,0:T(8,128)(2,1)S(1)} %bitcast.45), channel_id=1, replica_groups={{0,2,4,6,64,66,68,70,128,130,132,134,192,194,196,198},{1,3,5,7,65,67,69..., dimensions={0} | all-to-all | bytes 524288 | tf_op jit(solution)/shard_map/all_to_all | solution.py:139
  22.4 17.3 %all_to_all.61.tiles = bf16[8,8,1024]{2,1,0:T(8,128)(2,1)S(1)} all-to-all(bf16[8,8,1024]{2,1,0:T(8,128)(2,1)S(1)} %shard_map.77), channel_id=1, replica_groups={{0,8,16,24,32,40,48,56},{1,9,17,25,33,41,49,57},{2,10,18,26,34,42,50,58..., dimensions={0} | all-to-all | bytes 262144 | tf_op jit(solution)/shard_map/all_to_all | solution.py:139
  39.7 12.1 %all_to_all.62 = bf16[16,8,1024]{2,1,0:T(8,128)(2,1)S(1)} all-to-all(bf16[16,8,1024]{2,1,0:T(8,128)(2,1)S(1)} %shard_map.78), channel_id=1, replica_groups={{0,2,4,6,64,66,68,70,128,130,132,134,192,194,196,198},{1,3,5,7,65,67,69..., dimensions={0} | all-to-all | bytes 524288 | tf_op jit(solution)/shard_map/all_to_all | solution.py:139
  51.9 1.5 collective-permute-done.1.others
  53.4 2.4 %shard_map.79 = (f32[256,4096]{1,0:T(8,128)S(1)}, f32[256,128]{1,0:T(8,128)S(1)}) custom-call(bf16[128,1024]{1,0:T(8,128)(2,1)S(1)} %bitcast.44, bf16[128,1024]{1,0:T(8,128)(2,1)S(1)} %collective-permute-done.1.others, bf16[4096,1024]{1,0:T(8,128)(2,1)S(1)} %copy-done, f32[1,4096]{1,0:T(1,128)S(1)} %bitcast.63), custom_call_target="tpu_custom_call" | custom-call | tf_op jit(solution)/shard_map/pallas_call | solution.py:299
  55.8 17.9 %all_to_all.63 = f32[256,1,128]{2,1,0:T(1,128)S(1)} all-to-all(f32[256,1,128]{2,1,0:T(1,128)S(1)} %bitcast.62), channel_id=1, replica_groups={{0,1,3,2,4,5,7,6,70,71,69,68,66,67,65,64,128,129,131,130,132,133,135,13..., dimensions={0} | all-to-all | bytes 262144 | tf_op jit(solution)/shard_map/all_to_all | solution.py:139
  73.8 0.4 shard_map.80
  74.2 17.8 %all_to_all.64 = f32[256,1,128]{2,1,0:T(1,128)S(1)} all-to-all(f32[256,1,128]{2,1,0:T(1,128)S(1)} %bitcast.61), channel_id=1, replica_groups={{0,1,3,2,4,5,7,6,70,71,69,68,66,67,65,64,128,129,131,130,132,133,135,13..., dimensions={0} | all-to-all | bytes 262144 | tf_op jit(solution)/shard_map/all_to_all | solution.py:139
  92.5 17.8 %all_to_all.65 = f32[256,1,128]{2,1,0:T(1,128)S(1)} all-to-all(f32[256,1,128]{2,1,0:T(1,128)S(1)} %bitcast.55), channel_id=1, replica_groups={{0,1,3,2,4,5,7,6,70,71,69,68,66,67,65,64,128,129,131,130,132,133,135,13..., dimensions={0} | all-to-all | bytes 262144 | tf_op jit(solution)/shard_map/all_to_all | solution.py:139
  110.7 17.8 %all_to_all.66 = f32[256,1,128]{2,1,0:T(1,128)S(1)} all-to-all(f32[256,1,128]{2,1,0:T(1,128)S(1)} %bitcast.56), channel_id=1, replica_groups={{0,1,3,2,4,5,7,6,70,71,69,68,66,67,65,64,128,129,131,130,132,133,135,13..., dimensions={0} | all-to-all | bytes 262144 | tf_op jit(solution)/shard_map/all_to_all | solution.py:139
  129.0 18.0 %all_to_all.67 = f32[256,1,128]{2,1,0:T(1,128)S(1)} all-to-all(f32[256,1,128]{2,1,0:T(1,128)S(1)} %bitcast.57), channel_id=1, replica_groups={{0,1,3,2,4,5,7,6,70,71,69,68,66,67,65,64,128,129,131,130,132,133,135,13..., dimensions={0} | all-to-all | bytes 262144 | tf_op jit(solution)/shard_map/all_to_all | solution.py:139
  147.4 17.8 %all_to_all.68 = f32[256,1,128]{2,1,0:T(1,128)S(1)} all-to-all(f32[256,1,128]{2,1,0:T(1,128)S(1)} %bitcast.58), channel_id=1, replica_groups={{0,1,3,2,4,5,7,6,70,71,69,68,66,67,65,64,128,129,131,130,132,133,135,13..., dimensions={0} | all-to-all | bytes 262144 | tf_op jit(solution)/shard_map/all_to_all | solution.py:139
  165.7 17.8 %all_to_all.69 = f32[256,1,128]{2,1,0:T(1,128)S(1)} all-to-all(f32[256,1,128]{2,1,0:T(1,128)S(1)} %bitcast.59), channel_id=1, replica_groups={{0,1,3,2,4,5,7,6,70,71,69,68,66,67,65,64,128,129,131,130,132,133,135,13..., dimensions={0} | all-to-all | bytes 262144 | tf_op jit(solution)/shard_map/all_to_all | solution.py:139
  183.5 0.4 shard_map.86
  184.0 17.8 %all_to_all.70 = f32[256,1,128]{2,1,0:T(1,128)S(1)} all-to-all(f32[256,1,128]{2,1,0:T(1,128)S(1)} %bitcast.60), channel_id=1, replica_groups={{0,1,3,2,4,5,7,6,70,71,69,68,66,67,65,64,128,129,131,130,132,133,135,13..., dimensions={0} | all-to-all | bytes 262144 | tf_op jit(solution)/shard_map/all_to_all | solution.py:139
  201.8 1.0 shard_map.87
  202.8 6.6 %all-to-all-start.11 = ((f32[256,1,128]{2,1,0:T(1,128)}), f32[256,1,128]{2,1,0:T(1,128)S(1)}, u32[]{:S(2)}, u32[]{:S(2)}) async-start(f32[256,1,128]{2,1,0:T(1,128)} %bitcast.28), calls=%async_computation.11 | async-start | bytes 262144 | tf_op jit(solution)/shard_map/all_to_all | solution.py:139
  209.4 3.8 %shard_map.89 = f32[32,128]{1,0:T(8,128)} custom-call(s32[8,32]{1,0:T(8,128)S(1)} %copy-done.3, f32[8,128]{1,0:T(8,128)S(1)} %get-tuple-element.60.table, f32[32,128]{1,0:T(8,128)S(1)} %bitcast.65), custom_call_target="tpu_custom_call" | custom-call | tf_op jit(solution)/shard_map/pallas_call | solution.py:313
  213.2 7.8 %all-to-all-done.11 = f32[256,1,128]{2,1,0:T(1,128)S(1)} async-done(((f32[256,1,128]{2,1,0:T(1,128)}), f32[256,1,128]{2,1,0:T(1,128)S(1)}, u32[]{:S(2)}, u32[]{:S(2)}) %all-to-all-start.11) | async-done | bytes 131104 | tf_op jit(solution)/shard_map/all_to_all | solution.py:139
  221.0 0.6 shard_map.88
  (19 shorter events, 2.2 us)
Async XLA Ops:
  0.6 0.7 copy-start.2
  5.5 1.7 collective-permute-start
  39.7 13.7 %copy-start = (bf16[4096,1024]{1,0:T(8,128)(2,1)S(1)}, bf16[4096,1024]{1,0:T(8,128)(2,1)}, u32[]{:S(2)}) copy-start(bf16[4096,1024]{1,0:T(8,128)(2,1)} %points.3) | copy-start | bytes 25165828
  39.7 13.7 %copy-start.1 = (f32[4096]{0:T(1024)S(1)}, f32[4096]{0:T(1024)}, u32[]{:S(2)}) copy-start(f32[4096]{0:T(1024)} %param.5) | copy-start | bytes 49156
  51.9 1.5 collective-permute-start.1
  147.0 62.4 %copy-start.3 = (s32[8,32]{1,0:T(8,128)S(1)}, s32[8,32]{1,0:T(8,128)}, u32[]{:S(2)}) copy-start(s32[8,32]{1,0:T(8,128)} %proposals.3) | copy-start | bytes 3076
  147.0 62.4 %copy-start.4 = (f32[4096]{0:T(1024)S(1)}, f32[4096]{0:T(1024)}, u32[]{:S(2)}) copy-start(f32[4096]{0:T(1024)} %param.6) | copy-start | bytes 49156
  202.8 18.2 %all-to-all-start.11 = ((f32[256,1,128]{2,1,0:T(1,128)}), f32[256,1,128]{2,1,0:T(1,128)S(1)}, u32[]{:S(2)}, u32[]{:S(2)}) async-start(f32[256,1,128]{2,1,0:T(1,128)} %bitcast.28), calls=%async_computation.11 | async-start | bytes 262144 | tf_op jit(solution)/shard_map/all_to_all | solution.py:139

commit v3 on v2

--- a/solution.py
+++ b/solution.py
@@ -18,6 +18,7 @@
 GRANT = 12 << 20
 ROWS_GRANT = 46 << 20
 CHUNK = 512
+LISTS, SLOTS = 4, 4
 WAITS = pl.CostEstimate(flops=200_000_000_000, bytes_accessed=1_000_000_000, transcendentals=0)
 
 
@@ -33,7 +34,7 @@
     row_total = points.shape[0]
     steps, props = proposals.shape
     half = mine.shape[0]
-    lists, room = owned.shape
+    lists, slots = arrived.shape
     first = first_row(row_total)
 
     def offset_of(k):
@@ -49,31 +50,41 @@
                 found[part] += jnp.where((offset >= 0) & (offset < row_total), 1, 0)
         return tuple(found)
 
-    def copy(k):
+    def copy(k, part, slot):
         base = pl.multiple_of(lax.shift_right_logical(offset_of(k), 3) * SUB, SUB)
-        return pltpu.make_async_copy(points.at[pl.ds(base, SUB)], blocks.at[k], arrived.at[k])
+        return pltpu.make_async_copy(
+            points.at[pl.ds(base, SUB)], blocks.at[part, slot], arrived.at[part, slot]
+        )
 
     found = lax.fori_loop(0, steps // lists, note, (jnp.int32(0),) * lists)
-    for part in range(lists):
-
-        def start(i, carry, part=part):
-            copy(owned[part, i]).start()
-            return carry
-
-        lax.fori_loop(0, found[part], start, 0)
     rows[...] = jnp.zeros_like(rows)
-    for part in range(lists):
-
-        def take(i, carry, part=part):
-            k = owned[part, i]
-            copy(k).wait()
-            block = blocks[k].astype(jnp.float32)
-            line = lax.broadcasted_iota(jnp.int32, block.shape, 0)
-            row = jnp.where(line == (offset_of(k) & (SUB - 1)), block, 0.0)
-            rows[pl.ds(k, 1), :] = jnp.sum(row, axis=0, keepdims=True)
-            return carry
-
-        lax.fori_loop(0, found[part], take, 0)
+
+    def batch(b, carry):
+        done = b * slots
+        counts = [jnp.clip(found[part] - done, 0, slots) for part in range(lists)]
+        for part in range(lists):
+
+            def start(slot, carry, part=part):
+                copy(owned[part, done + slot], part, slot).start()
+                return carry
+
+            lax.fori_loop(0, counts[part], start, 0)
+        for part in range(lists):
+
+            def take(slot, carry, part=part):
+                k = owned[part, done + slot]
+                copy(k, part, slot).wait()
+                block = blocks[part, slot].astype(jnp.float32)
+                line = lax.broadcasted_iota(jnp.int32, block.shape, 0)
+                row = jnp.where(line == (offset_of(k) & (SUB - 1)), block, 0.0)
+                rows[pl.ds(k, 1), :] = jnp.sum(row, axis=0, keepdims=True)
+                return carry
+
+            lax.fori_loop(0, counts[part], take, 0)
+        return carry
+
+    longest = functools.reduce(jnp.maximum, found)
+    lax.fori_loop(0, lax.div(longest + slots - 1, slots), batch, 0)
     core = lax.rem(lax.axis_index(AXIS), CORES)
     at = pl.multiple_of(core * half, half)
     mine[...] = rows[pl.ds(at, half), :].astype(mine.dtype)
@@ -90,10 +101,10 @@
         in_specs=[SMEM, ANY],
         out_specs=[VMEM, VMEM],
         scratch_shapes=[
-            pltpu.SMEM((4, count // 4 + 1), jnp.int32),
-            pltpu.VMEM((count, SUB, width), points.dtype),
+            pltpu.SMEM((LISTS, count // LISTS + 1), jnp.int32),
+            pltpu.VMEM((LISTS, SLOTS, SUB, width), points.dtype),
             pltpu.VMEM((count, width), jnp.float32),
-            pltpu.SemaphoreType.DMA((count,)),
+            pltpu.SemaphoreType.DMA((LISTS, SLOTS)),
         ],
         compiler_params=pltpu.CompilerParams(vmem_limit_bytes=ROWS_GRANT),
     )(proposals, points)
@@ -163,11 +174,8 @@
     return tile
 
 
-def shares(gained, cover, props):
-    lane = lax.broadcasted_iota(jnp.int32, (1, LANES), 1)
-    row = as_row(jnp.sum(gained, axis=1, keepdims=True))
-    total = jnp.sum(cover[:1], axis=1, keepdims=True)
-    return jnp.where(lane == props, total, row)
+def shares(gained, cover):
+    return as_row(jnp.sum(jnp.concatenate([gained, cover], axis=0), axis=1, keepdims=True))
 
 
 def first_kernel(props, mine, others, points, best, similarity, out, fetched):
@@ -186,7 +194,7 @@
         for j in range(i, i + CHUNK, LANES):
             cols = slice(j, j + LANES)
             gained += jnp.maximum(similarity[0:props, cols] - best[:, cols], 0.0)
-    row = shares(gained, jnp.zeros((SUB, LANES), jnp.float32), props)
+    row = shares(gained, jnp.zeros((SUB, LANES), jnp.float32))
     out[...] = jnp.broadcast_to(row, out.shape)
 
 
@@ -198,25 +206,25 @@
     gains = jnp.sum(parts[...], axis=0, keepdims=True) / point_total
     new_table[...] = jnp.where(line == step, gains, table[...])
     total = jnp.sum(jnp.where(lane < props, gains, 0.0), axis=1, keepdims=True)
-    weight = as_column((gains + 0.01) / (total + 0.01 * props), props)
-    weights = jnp.broadcast_to(weight, (props, LANES))
+    whole = jnp.broadcast_to(1.0 / (total + 0.01 * props), (SUB, LANES))
+    share = jnp.broadcast_to(as_column(gains + 0.01, props), (props, LANES))
     here = slice(step * props, (step + 1) * props)
     following = slice((step + 1) * props, (step + 2) * props)
     gained = jnp.zeros((props, LANES), jnp.float32)
     cover = jnp.zeros((SUB, LANES), jnp.float32)
     for j in range(width // LANES):
         cols = slice(j * LANES, (j + 1) * LANES)
-        product = similarity[here, cols] * weights
+        product = similarity[here, cols] * share
         mixed = product[0:SUB]
         for i in range(SUB, props, SUB):
             mixed = mixed + product[i : i + SUB]
-        now = jnp.maximum(jnp.broadcast_to(best[:, cols], (SUB, LANES)), every_sublane(mixed))
+        now = jnp.maximum(jnp.broadcast_to(best[:, cols], (SUB, LANES)), every_sublane(mixed) * whole)
         new_best[:, cols] = now[: new_best.shape[0]]
         cover += now
         if not last:
             ahead = jnp.concatenate([now] * (props // SUB), axis=0)
             gained += jnp.maximum(similarity[following, cols] - ahead, 0.0)
-    return shares(gained, cover, props)
+    return shares(gained, cover)
 
 
 def middle_kernel(step, props, point_total, parts, similarity, best, table, new_best, new_table, out):
@@ -285,7 +293,7 @@
     steps, props = proposals.shape
     point_total = row_count * devices
 
-    mine, others = own_rows(proposals, embeddings)
+    mine, others = own_rows(pltpu.with_memory_space_constraint(proposals, pltpu.HBM), embeddings)
     half = shape_of(mine.shape, mine.dtype)
     tiles = call(pair_kernel, half, [VMEM] * 2)(mine, from_other_core(others))
     tiles = exchanged(tiles.reshape(X * Y, -1, mine.shape[1]), PLANES)

time: 225 us -> 221 us (0.982)
  Pallas kernels: 15 us -> 12.4 us
where the time goes in v3:
time: 221 us; the launch traced here: 218 us
  blocking collectives  188 us (85%)
  Pallas kernels  12.4 us (6%)
  waiting for transfers between devices  10.8 us (5%)
  starting transfers between devices  6.65 us (3%)
    all_to_all x11, blocking collectives, exchanged(): lax.all_to_all(tiles, AXIS, 0, 0, tiled=True, axis_index_groups=groups)  188 us
    all_to_all x1, waiting for transfers between devices, exchanged(): lax.all_to_all(tiles, AXIS, 0, 0, tiled=True, axis_index_groups=groups)  7.76 us
    all_to_all x1, starting transfers between devices, exchanged(): lax.all_to_all(tiles, AXIS, 0, 0, tiled=True, axis_index_groups=groups)  6.56 us
  transfers between devices with their start and end apart: 3, of which 3 were waited for; matrix products, arithmetic and copies ran while one was open for 0% of the time, Pallas kernels for 2%

profile of v3, /device:TPU:8, one launch (start us, length us, event | category | flops | bytes accessed | tf_op | source)
XLA Modules:
  0.0 218.4 jit_solution(10607668405659690373)
XLA Ops:
  0.6 2.1 shard_map.75
  2.8 1.5 collective-permute-done.arrived
  4.4 15.3 %all_to_all.60.tiles = bf16[16,8,1024]{2,1,0:T(8,128)(2,1)S(1)} all-to-all(bf16[16,8,1024]{2,1,0:T(8,128)(2,1)S(1)} %bitcast.45), channel_id=1, replica_groups={{0,2,4,6,64,66,68,70,128,130,132,134,192,194,196,198},{1,3,5,7,65,67,69..., dimensions={0} | all-to-all | bytes 524288 | tf_op jit(solution)/shard_map/all_to_all | solution.py:150
  19.7 17.3 %all_to_all.61.tiles = bf16[8,8,1024]{2,1,0:T(8,128)(2,1)S(1)} all-to-all(bf16[8,8,1024]{2,1,0:T(8,128)(2,1)S(1)} %shard_map.77), channel_id=1, replica_groups={{0,8,16,24,32,40,48,56},{1,9,17,25,33,41,49,57},{2,10,18,26,34,42,50,58..., dimensions={0} | all-to-all | bytes 262144 | tf_op jit(solution)/shard_map/all_to_all | solution.py:150
  37.1 12.1 %all_to_all.62 = bf16[16,8,1024]{2,1,0:T(8,128)(2,1)S(1)} all-to-all(bf16[16,8,1024]{2,1,0:T(8,128)(2,1)S(1)} %shard_map.78), channel_id=1, replica_groups={{0,2,4,6,64,66,68,70,128,130,132,134,192,194,196,198},{1,3,5,7,65,67,69..., dimensions={0} | all-to-all | bytes 524288 | tf_op jit(solution)/shard_map/all_to_all | solution.py:150
  49.2 1.5 collective-permute-done.1.others
  50.8 2.4 %shard_map.79 = (f32[256,4096]{1,0:T(8,128)S(1)}, f32[256,128]{1,0:T(8,128)S(1)}) custom-call(bf16[128,1024]{1,0:T(8,128)(2,1)S(1)} %bitcast.44, bf16[128,1024]{1,0:T(8,128)(2,1)S(1)} %collective-permute-done.1.others, bf16[4096,1024]{1,0:T(8,128)(2,1)S(1)} %copy-done, f32[1,4096]{1,0:T(1,128)S(1)} %bitcast.63), custom_call_target="tpu_custom_call" | custom-call | tf_op jit(solution)/shard_map/pallas_call | solution.py:307
  53.2 18.0 %all_to_all.63 = f32[256,1,128]{2,1,0:T(1,128)S(1)} all-to-all(f32[256,1,128]{2,1,0:T(1,128)S(1)} %bitcast.62), channel_id=1, replica_groups={{0,1,3,2,4,5,7,6,70,71,69,68,66,67,65,64,128,129,131,130,132,133,135,13..., dimensions={0} | all-to-all | bytes 262144 | tf_op jit(solution)/shard_map/all_to_all | solution.py:150
  71.1 0.3 shard_map.80
  71.5 17.8 %all_to_all.64 = f32[256,1,128]{2,1,0:T(1,128)S(1)} all-to-all(f32[256,1,128]{2,1,0:T(1,128)S(1)} %bitcast.61), channel_id=1, replica_groups={{0,1,3,2,4,5,7,6,70,71,69,68,66,67,65,64,128,129,131,130,132,133,135,13..., dimensions={0} | all-to-all | bytes 262144 | tf_op jit(solution)/shard_map/all_to_all | solution.py:150
  89.3 0.3 shard_map.81
  89.7 17.8 %all_to_all.65 = f32[256,1,128]{2,1,0:T(1,128)S(1)} all-to-all(f32[256,1,128]{2,1,0:T(1,128)S(1)} %bitcast.55), channel_id=1, replica_groups={{0,1,3,2,4,5,7,6,70,71,69,68,66,67,65,64,128,129,131,130,132,133,135,13..., dimensions={0} | all-to-all | bytes 262144 | tf_op jit(solution)/shard_map/all_to_all | solution.py:150
  107.9 17.8 %all_to_all.66 = f32[256,1,128]{2,1,0:T(1,128)S(1)} all-to-all(f32[256,1,128]{2,1,0:T(1,128)S(1)} %bitcast.56), channel_id=1, replica_groups={{0,1,3,2,4,5,7,6,70,71,69,68,66,67,65,64,128,129,131,130,132,133,135,13..., dimensions={0} | all-to-all | bytes 262144 | tf_op jit(solution)/shard_map/all_to_all | solution.py:150
  126.0 18.0 %all_to_all.67 = f32[256,1,128]{2,1,0:T(1,128)S(1)} all-to-all(f32[256,1,128]{2,1,0:T(1,128)S(1)} %bitcast.57), channel_id=1, replica_groups={{0,1,3,2,4,5,7,6,70,71,69,68,66,67,65,64,128,129,131,130,132,133,135,13..., dimensions={0} | all-to-all | bytes 262144 | tf_op jit(solution)/shard_map/all_to_all | solution.py:150
  144.4 17.8 %all_to_all.68 = f32[256,1,128]{2,1,0:T(1,128)S(1)} all-to-all(f32[256,1,128]{2,1,0:T(1,128)S(1)} %bitcast.58), channel_id=1, replica_groups={{0,1,3,2,4,5,7,6,70,71,69,68,66,67,65,64,128,129,131,130,132,133,135,13..., dimensions={0} | all-to-all | bytes 262144 | tf_op jit(solution)/shard_map/all_to_all | solution.py:150
  162.2 0.3 shard_map.85
  162.6 17.8 %all_to_all.69 = f32[256,1,128]{2,1,0:T(1,128)S(1)} all-to-all(f32[256,1,128]{2,1,0:T(1,128)S(1)} %bitcast.59), channel_id=1, replica_groups={{0,1,3,2,4,5,7,6,70,71,69,68,66,67,65,64,128,129,131,130,132,133,135,13..., dimensions={0} | all-to-all | bytes 262144 | tf_op jit(solution)/shard_map/all_to_all | solution.py:150
  180.4 0.3 shard_map.86
  180.8 17.8 %all_to_all.70 = f32[256,1,128]{2,1,0:T(1,128)S(1)} all-to-all(f32[256,1,128]{2,1,0:T(1,128)S(1)} %bitcast.60), channel_id=1, replica_groups={{0,1,3,2,4,5,7,6,70,71,69,68,66,67,65,64,128,129,131,130,132,133,135,13..., dimensions={0} | all-to-all | bytes 262144 | tf_op jit(solution)/shard_map/all_to_all | solution.py:150
  198.6 1.0 shard_map.87
  199.6 6.6 %all-to-all-start.11 = ((f32[256,1,128]{2,1,0:T(1,128)}), f32[256,1,128]{2,1,0:T(1,128)S(1)}, u32[]{:S(2)}, u32[]{:S(2)}) async-start(f32[256,1,128]{2,1,0:T(1,128)} %bitcast.28), calls=%async_computation.11 | async-start | bytes 262144 | tf_op jit(solution)/shard_map/all_to_all | solution.py:150
  206.2 3.8 %shard_map.89 = f32[32,128]{1,0:T(8,128)} custom-call(s32[8,32]{1,0:T(8,128)S(1)} %copy-done.2, f32[8,128]{1,0:T(8,128)S(1)} %get-tuple-element.60.table, f32[32,128]{1,0:T(8,128)S(1)} %bitcast.65), custom_call_target="tpu_custom_call" | custom-call | tf_op jit(solution)/shard_map/pallas_call | solution.py:321
  210.0 7.8 %all-to-all-done.11 = f32[256,1,128]{2,1,0:T(1,128)S(1)} async-done(((f32[256,1,128]{2,1,0:T(1,128)}), f32[256,1,128]{2,1,0:T(1,128)S(1)}, u32[]{:S(2)}, u32[]{:S(2)}) %all-to-all-start.11) | async-done | bytes 131104 | tf_op jit(solution)/shard_map/all_to_all | solution.py:150
  217.7 0.6 shard_map.88
  (17 shorter events, 1.2 us)
Async XLA Ops:
  2.7 1.6 collective-permute-start
  37.0 13.7 %copy-start = (bf16[4096,1024]{1,0:T(8,128)(2,1)S(1)}, bf16[4096,1024]{1,0:T(8,128)(2,1)}, u32[]{:S(2)}) copy-start(bf16[4096,1024]{1,0:T(8,128)(2,1)} %points.3) | copy-start | bytes 25165828
  37.0 13.7 %copy-start.1 = (f32[4096]{0:T(1024)S(1)}, f32[4096]{0:T(1024)}, u32[]{:S(2)}) copy-start(f32[4096]{0:T(1024)} %param.5) | copy-start | bytes 49156
  49.2 1.5 collective-permute-start.1
  144.1 62.1 %copy-start.2 = (s32[8,32]{1,0:T(8,128)S(1)}, s32[8,32]{1,0:T(8,128)}, u32[]{:S(2)}) copy-start(s32[8,32]{1,0:T(8,128)} %proposals.3) | copy-start | bytes 3076
  144.1 62.1 %copy-start.3 = (f32[4096]{0:T(1024)S(1)}, f32[4096]{0:T(1024)}, u32[]{:S(2)}) copy-start(f32[4096]{0:T(1024)} %param.6) | copy-start | bytes 49156
  199.6 18.2 %all-to-all-start.11 = ((f32[256,1,128]{2,1,0:T(1,128)}), f32[256,1,128]{2,1,0:T(1,128)S(1)}, u32[]{:S(2)}, u32[]{:S(2)}) async-start(f32[256,1,128]{2,1,0:T(1,128)} %bitcast.28), calls=%async_computation.11 | async-start | bytes 262144 | tf_op jit(solution)/shard_map/all_to_all | solution.py:150
